TPU v7x, 32 devices: a whole 2x2x4 slice. The times are simulated.
32 devices in a mesh: dp: 2 (over x), crop: 4 (over y, core), tensor: 4 (over z).
Axes of the slice: x: 2, y: 2, z: 4, core: 2. Of those that a mesh axis runs over, the one named last changes fastest.
Arguments:
- hidden_a: bfloat16 [512, 8192], P('crop', 'dp'), as said below
- hidden_b: bfloat16 [512, 8192], P('crop', 'dp'), as said below
- weight: bfloat16 [8192, 8192], P('dp', 'tensor')
Outputs:
- weight_grad: float32 [8192, 8192], P(('dp', 'crop'), 'tensor')
Inputs may be any that keep to these rules, and one draw needn't show every extreme that they name: `hidden_a`: nonnegative entries. `hidden_b`: nonnegative entries.
All inputs are finite; a program needn't handle non-finite values.
Results may differ from a plain program's by a relative error of at most 0.0015.
Values may be sent and summed in bfloat16 or wider, within the bound.
A program may use at most 128 MiB of HBM per device.

v0:
```python
import jax
import jax.numpy as jnp
from jax import lax
from jax.sharding import PartitionSpec as P

epsilon = 0.0001


def body(hidden_a, hidden_b, weight):
    group_size = lax.axis_size(("dp", "crop"))
    data_count = lax.axis_size("dp")
    block_rows = hidden_a.shape[0]
    local_rows = block_rows // data_count
    total_rows = local_rows * group_size
    left_part = jnp.dot(hidden_a, weight, preferred_element_type=jnp.float32)
    right_part = jnp.dot(hidden_b, weight, preferred_element_type=jnp.float32)
    joined = lax.psum_scatter(
        jnp.stack([left_part, right_part], axis=1), "dp", scatter_dimension=0, tiled=True
    ).astype(jnp.bfloat16)
    stacked = jnp.stack([joined[:, 0, :], joined[:, 1, :]]).astype(jnp.float32)
    col_means = lax.psum(jnp.sum(stacked, axis=1), ("dp", "crop")) / total_rows
    centered = stacked - col_means[:, None, :]
    spread = lax.psum(jnp.sum(centered * centered, axis=1), ("dp", "crop"))
    deviation = jnp.sqrt(spread / (total_rows - 1.0) + epsilon)
    rounded = centered.astype(jnp.bfloat16)
    everyone = lax.all_gather(rounded, ("dp", "crop"), axis=1, tiled=True)
    gram = jnp.einsum("vrf,vbf->vrb", rounded, everyone, preferred_element_type=jnp.float32)
    gram = lax.psum(gram, "tensor")
    gram_low = gram.astype(jnp.bfloat16)
    products = jnp.einsum("vrb,vbf->vrf", gram_low, everyone, preferred_element_type=jnp.float32)
    hinge_rate = jnp.where(deviation < 1.0, 25.0 / ((total_rows - 1.0) * deviation), 0.0)[
        :, None, :
    ]
    differ = stacked[0] - stacked[1]
    pull_term = jnp.stack([differ, -differ]) * (50.0 / total_rows)
    cov_scale = 4.0 / (total_rows - 1.0) ** 2
    row_grads = (
        pull_term - hinge_rate * centered + cov_scale * (products - centered * spread[:, None, :])
    )
    row_grads = row_grads.astype(jnp.bfloat16)
    block_grads = lax.all_gather(row_grads, "dp", axis=1, tiled=True)
    across = (((0,), (0,)), ((), ()))
    left_part = lax.dot_general(
        hidden_a, block_grads[0], across, preferred_element_type=jnp.float32
    )
    right_part = lax.dot_general(
        hidden_b, block_grads[1], across, preferred_element_type=jnp.float32
    )
    return lax.psum_scatter(left_part + right_part, "crop", scatter_dimension=0, tiled=True)


def solution(mesh):
    placed = (P("crop", "dp"), P("crop", "dp"), P("dp", "tensor"))
    return jax.shard_map(
        body, mesh=mesh, in_specs=placed, out_specs=P(("dp", "crop"), "tensor"), check_vma=False
    )
```

profile of v0, /device:TPU:0, one launch (start us, length us, event | category | flops | bytes accessed | tf_op | source)
XLA Modules:
  0.0 458.1 jit_solution(6418926525455714938)
XLA Ops:
  6.5 1.2 copy-done
  7.8 8.2 %convolution_bitcast_fusion.1 = f32[128,1,2048]{2,0,1:T(8,128)S(1)} fusion(bf16[128,4096]{1,0:T(8,128)(2,1)S(1)} %copy-done, bf16[4096,2048]{1,0:T(8,128)(2,1)} %param.5), kind=kOutput, calls=%fused_computation.5 | convolution fusion | flops 2147483648 | bytes 18874368 | tf_op jit(solution)/shard_map/dot_general | solution.py:15
  16.0 2.4 copy-done.2
  18.4 2.4 convolution_bitcast_fusion
  20.8 1.5 pad_maximum_fusion
  22.3 34.7 %reduce-scatter.3.cloned.1.call-done = f32[64,2,2048]{2,0,1:T(8,128)} async-done(((f32[128,2,2048]{2,0,1:T(8,128)}), f32[64,2,2048]{2,0,1:T(8,128)}) %reduce-scatter.3.cloned.1.call-update) | async-done | bytes 1048592 | tf_op jit(solution)/shard_map/reduce_scatter | solution.py:17
  57.1 1.3 convert_element_type.15
  58.4 0.1 convert_reduce_fusion
  58.5 22.9 %psum.21 = f32[2,2048]{1,0:T(2,128)S(1)} all-reduce(f32[2,2048]{1,0:T(2,128)S(1)} %convert_reduce_fusion), channel_id=1, replica_groups=mesh['dp'=2,'crop'=4,'tensor'=4] {'dp','crop'}, use_global_device_ids=true, to_apply=%region_2.0 | all-reduce | flops 4096 | bytes 32768 | tf_op jit(solution)/shard_map/psum | solution.py:21
  81.5 1.0 multiply_reduce_fusion
  82.5 22.7 %psum.22 = f32[2,2048]{1,0:T(2,128)S(1)} all-reduce(f32[2,2048]{1,0:T(2,128)S(1)} %get-tuple-element.7), channel_id=1, replica_groups=mesh['dp'=2,'crop'=4,'tensor'=4] {'dp','crop'}, use_global_device_ids=true, to_apply=%region_4.0 | all-reduce | flops 4096 | bytes 32768 | tf_op jit(solution)/shard_map/psum | solution.py:23
  105.3 0.5 copy-done.5
  105.8 0.6 compare_select_fusion
  106.4 0.9 fusion.7
  107.3 12.0 %all-gather.3.cloned.1.call-done = bf16[2,512,2048]{2,1,0:T(8,128)(2,1)} async-done(((bf16[2,64,2048]{2,1,0:T(8,128)(2,1)}), bf16[2,512,2048]{2,1,0:T(8,128)(2,1)}) %all-gather.3.cloned.1.call-update) | async-done | bytes 4194320 | tf_op jit(solution)/shard_map/all_gather | solution.py:26
  119.3 3.7 fusion.8
  123.1 24.7 %all-reduce.1 = bf16[2,64,512]{2,1,0:T(8,128)(2,1)S(1)} all-reduce(f32[2,64,512]{2,1,0:T(8,128)S(1)} %fusion.8), channel_id=1, replica_groups=mesh['dp'=2,'crop'=4,'tensor'=4] {'tensor'}, use_global_device_ids=true, to_apply=%region_5.0 | all-reduce | flops 65536 | bytes 393216 | tf_op jit(solution)/shard_map/psum | solution.py:28
  147.7 4.2 fusion.2
  152.0 0.2 reduce-scatter.5.cloned.1.call-start
  152.2 18.8 %all-gather.5.cloned.1.call-done = bf16[2,128,2048]{2,1,0:T(8,128)(2,1)} async-done(((bf16[2,64,2048]{2,1,0:T(8,128)(2,1)}), bf16[2,128,2048]{2,1,0:T(8,128)(2,1)}) %all-gather.5.cloned.1.call-update) | async-done | bytes 1048592 | tf_op jit(solution)/shard_map/all_gather | solution.py:41
  171.0 14.3 %fusion.4 = f32[2048,4096]{1,0:T(8,128)} fusion(bf16[128,4096]{1,0:T(8,128)(2,1)S(1)} %copy-done, bf16[2,128,2048]{2,1,0:T(8,128)(2,1)} %all-gather.5.cloned.1.call-done), kind=kOutput, calls=%fused_computation.15 | convolution fusion | flops 2147483648 | bytes 35127296 | tf_op jit(solution)/shard_map/dot_general | solution.py:43
  185.3 24.8 %add_bitcast_fusion = f32[4096,2048]{0,1:T(8,128)} fusion(f32[2048,4096]{1,0:T(8,128)} %fusion.4, bf16[128,4096]{1,0:T(8,128)(2,1)S(1)} %copy-done.3, bf16[2,128,2048]{2,1,0:T(8,128)(2,1)S(1)} %copy-done.4), kind=kOutput, calls=%fused_computation | convolution fusion | flops 2155872256 | bytes 68681728 | tf_op jit(solution)/shard_map/dot_general | solution.py:46
  210.1 232.3 %reduce-scatter.5.cloned.1.call-done = f32[1024,2048]{0,1:T(8,128)} async-done(((f32[4096,2048]{0,1:T(8,128)}), f32[1024,2048]{0,1:T(8,128)}) %reduce-scatter.5.cloned.1.call-update) | async-done | bytes 8388624 | tf_op jit(solution)/shard_map/reduce_scatter | solution.py:49
  442.4 9.1 %copy.4 = f32[1024,2048]{1,0:T(8,128)} copy(f32[1024,2048]{0,1:T(8,128)} %reduce-scatter.5.cloned.1.call-done) | data formatting | bytes 16777216 | tf_op jit(solution)/shard_map/reduce_scatter | solution.py:49
  (19 shorter events, 0.3 us)
Async XLA Ops:
  6.5 1.2 copy-start
  6.5 9.5 %copy-start.3 = (bf16[128,4096]{1,0:T(8,128)(2,1)S(1)}, bf16[128,4096]{1,0:T(8,128)(2,1)}, u32[]{:S(2)}) copy-start(bf16[128,4096]{1,0:T(8,128)(2,1)} %param.4) | copy-start | bytes 3145732
  6.5 50.5 %reduce-scatter.3.cloned.1.call-start = ((), (), s32[]{:S(2)}) async-start(), calls=%async_computation.2 | async-start | bytes 3145728 | tf_op jit(solution)/shard_map/reduce_scatter | solution.py:17
  7.8 10.6 %copy-start.2 = (bf16[4096,2048]{1,0:T(8,128)(2,1)S(1)}, bf16[4096,2048]{1,0:T(8,128)(2,1)}, u32[]{:S(2)}) copy-start(bf16[4096,2048]{1,0:T(8,128)(2,1)} %param.5) | copy-start | bytes 50331652
  22.3 97.0 %all-gather.3.cloned.1.call-start = ((), (), s32[]{:S(2)}) async-start(), calls=%async_computation.3 | async-start | bytes 4718592 | tf_op jit(solution)/shard_map/all_gather | solution.py:26
  82.4 88.5 %all-gather.5.cloned.1.call-start = ((), (), s32[]{:S(2)}) async-start(), calls=%async_computation.4 | async-start | bytes 1572864 | tf_op jit(solution)/shard_map/all_gather | solution.py:41
  105.2 0.6 copy-start.5
  152.0 290.4 %reduce-scatter.5.cloned.1.call-start = ((), (), s32[]{:S(2)}) async-start(), calls=%async_computation.5 | async-start | bytes 41943040 | tf_op jit(solution)/shard_map/reduce_scatter | solution.py:49
  171.0 14.3 %copy-start.4 = (bf16[2,128,2048]{2,1,0:T(8,128)(2,1)S(1)}, bf16[2,128,2048]{2,1,0:T(8,128)(2,1)}, u32[]{:S(2)}) copy-start(bf16[2,128,2048]{2,1,0:T(8,128)(2,1)} %all-gather.5.cloned.1.call-done) | copy-start | bytes 3145732
  210.1 241.5 %copy-start.1 = (bf16[128,4096]{1,0:T(8,128)(2,1)S(1)}, bf16[128,4096]{1,0:T(8,128)(2,1)}, u32[]{:S(2)}) copy-start(bf16[128,4096]{1,0:T(8,128)(2,1)} %param.3) | copy-start | bytes 3145732
Sparse Core Ops, SparseCore 0:
  22.4 34.6 reduce-scatter.2
  82.6 36.6 all-gather.2
  152.1 18.8 all-gather.4
  210.2 232.1 reduce-scatter.4
where the time goes:
time: 458 us
  waiting for transfers between devices  298 us (65%)
  blocking collectives  70.3 us (15%)
  matrix products  57.7 us (13%)
  local copies, waits for them, and re-layouts  13.3 us (3%)
  between operations  13.2 us (3%)
  other arithmetic  5.43 us (1%)
    reduce_scatter x1, waiting for transfers between devices, body(): lax.psum_scatter(left_part + right_part, 'crop', scatter_dimension=0, til...  232 us
    reduce_scatter x1, waiting for transfers between devices, body(): lax.psum_scatter(jnp.stack([left_part, right_part], axis=1), 'dp', scatte...  34.7 us
    dot_general x1, matrix products, body(): lax.dot_general(hidden_b, block_grads[1], across, preferred_element_type=...  24.8 us
    psum x1, blocking collectives, body(): gram = lax.psum(gram, 'tensor')  24.7 us
    psum x1, blocking collectives, body(): col_means = lax.psum(jnp.sum(stacked, axis=1), ('dp', 'crop')) / total_rows  22.9 us
    psum x1, blocking collectives, body(): spread = lax.psum(jnp.sum(centered * centered, axis=1), ('dp', 'crop'))  22.7 us
    all_gather x1, waiting for transfers between devices, body(): block_grads = lax.all_gather(row_grads, 'dp', axis=1, tiled=True)  18.8 us
    dot_general x1, matrix products, body(): lax.dot_general(hidden_a, block_grads[0], across, preferred_element_type=...  14.3 us
  transfers between devices with their start and end apart: 4, of which 4 were waited for; matrix products, arithmetic and copies ran while one was open for 0% of the time, Pallas kernels for 0%

commit v1 on v0

--- a/solution.py
+++ b/solution.py
@@ -18,7 +18,9 @@
         jnp.stack([left_part, right_part], axis=1), "dp", scatter_dimension=0, tiled=True
     ).astype(jnp.bfloat16)
     stacked = jnp.stack([joined[:, 0, :], joined[:, 1, :]]).astype(jnp.float32)
-    col_means = lax.psum(jnp.sum(stacked, axis=1), ("dp", "crop")) / total_rows
+    col_means = (
+        jnp.sum(lax.all_gather(jnp.sum(stacked, axis=1), ("dp", "crop")), axis=0) / total_rows
+    )
     centered = stacked - col_means[:, None, :]
     spread = lax.psum(jnp.sum(centered * centered, axis=1), ("dp", "crop"))
     deviation = jnp.sqrt(spread / (total_rows - 1.0) + epsilon)

time: 458 us -> 445 us (0.972)
  blocking collectives: 70.3 us -> 57.9 us
    psum x1 -> x0, blocking collectives: 22.9 us -> none  [body(): col_means = lax.psum(jnp.sum(stacked, axis=1), ('dp', 'crop')) / total_rows]
    all_gather x0 -> x1, blocking collectives: none -> 9.19 us  [body(): lax.all_gather(jnp.sum(stacked, axis=1), ('dp', 'crop'))]
where the time goes in v1:
time: 445 us; the launch traced here: 444 us
  waiting for transfers between devices  297 us (67%)
  blocking collectives  57.9 us (13%)
  matrix products  57.7 us (13%)
  local copies, waits for them, and re-layouts  13.3 us (3%)
  between operations  13.2 us (3%)
  other arithmetic  5.48 us (1%)
    reduce_scatter x1, waiting for transfers between devices, body(): lax.psum_scatter(left_part + right_part, 'crop', scatter_dimension=0, til...  232 us
    reduce_scatter x1, waiting for transfers between devices, body(): lax.psum_scatter(jnp.stack([left_part, right_part], axis=1), 'dp', scatte...  34.7 us
    dot_general x1, matrix products, body(): lax.dot_general(hidden_b, block_grads[1], across, preferred_element_type=...  24.8 us
    psum x1, blocking collectives, body(): gram = lax.psum(gram, 'tensor')  24.7 us
    psum x1, blocking collectives, body(): spread = lax.psum(jnp.sum(centered * centered, axis=1), ('dp', 'crop'))  24.1 us
    all_gather x1, waiting for transfers between devices, body(): block_grads = lax.all_gather(row_grads, 'dp', axis=1, tiled=True)  18.7 us
    dot_general x1, matrix products, body(): lax.dot_general(hidden_a, block_grads[0], across, preferred_element_type=...  14.3 us
    all_gather x1, waiting for transfers between devices, body(): everyone = lax.all_gather(rounded, ('dp', 'crop'), axis=1, tiled=True)  10.7 us
  transfers between devices with their start and end apart: 4, of which 4 were waited for; matrix products, arithmetic and copies ran while one was open for 0% of the time, Pallas kernels for 0%

profile of v1, /device:TPU:0, one launch (start us, length us, event | category | flops | bytes accessed | tf_op | source)
XLA Modules:
  0.0 444.4 jit_solution(5862508707806952413)
XLA Ops:
  6.5 1.2 copy-done
  7.8 8.2 %convolution_bitcast_fusion.1 = f32[128,1,2048]{2,0,1:T(8,128)S(1)} fusion(bf16[128,4096]{1,0:T(8,128)(2,1)S(1)} %copy-done, bf16[4096,2048]{1,0:T(8,128)(2,1)} %param.5), kind=kOutput, calls=%fused_computation.5 | convolution fusion | flops 2147483648 | bytes 18874368 | tf_op jit(solution)/shard_map/dot_general | solution.py:15
  16.0 2.4 copy-done.2
  18.4 2.4 convolution_bitcast_fusion
  20.8 1.5 pad_maximum_fusion
  22.3 34.7 %reduce-scatter.3.cloned.1.call-done = f32[64,2,2048]{2,0,1:T(8,128)} async-done(((f32[128,2,2048]{2,0,1:T(8,128)}), f32[64,2,2048]{2,0,1:T(8,128)}) %reduce-scatter.3.cloned.1.call-update) | async-done | bytes 1048592 | tf_op jit(solution)/shard_map/reduce_scatter | solution.py:17
  57.1 1.3 convert_element_type.15
  58.4 0.1 convert_reduce_fusion
  58.5 9.2 %all-gather.1 = f32[8,2,2048]{2,1,0:T(2,128)S(1)} all-gather(f32[1,2,2048]{2,1,0:T(2,128)S(1)} %bitcast.27), channel_id=2, replica_groups=mesh['dp'=2,'crop'=4,'tensor'=4] {'dp','crop'}, dimensions={0}, use_global_device_ids=true | all-gather | bytes 147456 | tf_op jit(solution)/shard_map/all_gather | solution.py:22
  67.8 1.0 multiply_reduce_fusion
  68.8 24.1 %psum.14 = f32[2,2048]{1,0:T(2,128)S(1)} all-reduce(f32[2,2048]{1,0:T(2,128)S(1)} %get-tuple-element.7), channel_id=1, replica_groups=mesh['dp'=2,'crop'=4,'tensor'=4] {'dp','crop'}, use_global_device_ids=true, to_apply=%region_4.0 | all-reduce | flops 4096 | bytes 32768 | tf_op jit(solution)/shard_map/psum | solution.py:25
  92.9 0.5 copy-done.5
  93.5 0.6 compare_select_fusion
  94.1 0.9 fusion.7
  95.0 10.7 %all-gather.5.cloned.1.call-done = bf16[2,512,2048]{2,1,0:T(8,128)(2,1)} async-done(((bf16[2,64,2048]{2,1,0:T(8,128)(2,1)}), bf16[2,512,2048]{2,1,0:T(8,128)(2,1)}) %all-gather.5.cloned.1.call-update) | async-done | bytes 4194320 | tf_op jit(solution)/shard_map/all_gather | solution.py:28
  105.7 3.7 fusion.8
  109.4 24.7 %all-reduce.1 = bf16[2,64,512]{2,1,0:T(8,128)(2,1)S(1)} all-reduce(f32[2,64,512]{2,1,0:T(8,128)S(1)} %fusion.8), channel_id=1, replica_groups=mesh['dp'=2,'crop'=4,'tensor'=4] {'tensor'}, use_global_device_ids=true, to_apply=%region_5.0 | all-reduce | flops 65536 | bytes 393216 | tf_op jit(solution)/shard_map/psum | solution.py:30
  134.1 4.2 fusion.2
  138.4 0.2 reduce-scatter.5.cloned.1.call-start
  138.6 18.7 %all-gather.7.cloned.1.call-done = bf16[2,128,2048]{2,1,0:T(8,128)(2,1)} async-done(((bf16[2,64,2048]{2,1,0:T(8,128)(2,1)}), bf16[2,128,2048]{2,1,0:T(8,128)(2,1)}) %all-gather.7.cloned.1.call-update) | async-done | bytes 1048592 | tf_op jit(solution)/shard_map/all_gather | solution.py:43
  157.3 14.3 %fusion.4 = f32[2048,4096]{1,0:T(8,128)} fusion(bf16[128,4096]{1,0:T(8,128)(2,1)S(1)} %copy-done, bf16[2,128,2048]{2,1,0:T(8,128)(2,1)} %all-gather.7.cloned.1.call-done), kind=kOutput, calls=%fused_computation.15 | convolution fusion | flops 2147483648 | bytes 35127296 | tf_op jit(solution)/shard_map/dot_general | solution.py:45
  171.6 24.8 %add_bitcast_fusion = f32[4096,2048]{0,1:T(8,128)} fusion(f32[2048,4096]{1,0:T(8,128)} %fusion.4, bf16[128,4096]{1,0:T(8,128)(2,1)S(1)} %copy-done.3, bf16[2,128,2048]{2,1,0:T(8,128)(2,1)S(1)} %copy-done.4), kind=kOutput, calls=%fused_computation | convolution fusion | flops 2155872256 | bytes 68681728 | tf_op jit(solution)/shard_map/dot_general | solution.py:48
  196.4 232.3 %reduce-scatter.5.cloned.1.call-done = f32[1024,2048]{0,1:T(8,128)} async-done(((f32[4096,2048]{0,1:T(8,128)}), f32[1024,2048]{0,1:T(8,128)}) %reduce-scatter.5.cloned.1.call-update) | async-done | bytes 8388624 | tf_op jit(solution)/shard_map/reduce_scatter | solution.py:51
  428.8 9.1 %copy.5 = f32[1024,2048]{1,0:T(8,128)} copy(f32[1024,2048]{0,1:T(8,128)} %reduce-scatter.5.cloned.1.call-done) | data formatting | bytes 16777216 | tf_op jit(solution)/shard_map/reduce_scatter | solution.py:51
  (20 shorter events, 0.3 us)
Async XLA Ops:
  6.5 1.2 copy-start
  6.5 9.5 %copy-start.3 = (bf16[128,4096]{1,0:T(8,128)(2,1)S(1)}, bf16[128,4096]{1,0:T(8,128)(2,1)}, u32[]{:S(2)}) copy-start(bf16[128,4096]{1,0:T(8,128)(2,1)} %param.4) | copy-start | bytes 3145732
  6.5 50.5 %reduce-scatter.3.cloned.1.call-start = ((), (), s32[]{:S(2)}) async-start(), calls=%async_computation.2 | async-start | bytes 3145728 | tf_op jit(solution)/shard_map/reduce_scatter | solution.py:17
  7.8 10.6 %copy-start.2 = (bf16[4096,2048]{1,0:T(8,128)(2,1)S(1)}, bf16[4096,2048]{1,0:T(8,128)(2,1)}, u32[]{:S(2)}) copy-start(bf16[4096,2048]{1,0:T(8,128)(2,1)} %param.5) | copy-start | bytes 50331652
  22.3 83.4 %all-gather.5.cloned.1.call-start = ((), (), s32[]{:S(2)}) async-start(), calls=%async_computation.3 | async-start | bytes 4718592 | tf_op jit(solution)/shard_map/all_gather | solution.py:28
  68.8 88.6 %all-gather.7.cloned.1.call-start = ((), (), s32[]{:S(2)}) async-start(), calls=%async_computation.4 | async-start | bytes 1572864 | tf_op jit(solution)/shard_map/all_gather | solution.py:43
  92.9 0.6 copy-start.5
  138.4 290.4 %reduce-scatter.5.cloned.1.call-start = ((), (), s32[]{:S(2)}) async-start(), calls=%async_computation.5 | async-start | bytes 41943040 | tf_op jit(solution)/shard_map/reduce_scatter | solution.py:51
  157.3 14.3 %copy-start.4 = (bf16[2,128,2048]{2,1,0:T(8,128)(2,1)S(1)}, bf16[2,128,2048]{2,1,0:T(8,128)(2,1)}, u32[]{:S(2)}) copy-start(bf16[2,128,2048]{2,1,0:T(8,128)(2,1)} %all-gather.7.cloned.1.call-done) | copy-start | bytes 3145732
  196.4 241.5 %copy-start.1 = (bf16[128,4096]{1,0:T(8,128)(2,1)S(1)}, bf16[128,4096]{1,0:T(8,128)(2,1)}, u32[]{:S(2)}) copy-start(bf16[128,4096]{1,0:T(8,128)(2,1)} %param.3) | copy-start | bytes 3145732
Sparse Core Ops, SparseCore 0:
  22.4 34.6 reduce-scatter.2
  68.9 36.7 all-gather.4
  138.5 18.8 all-gather.6
  196.5 232.1 reduce-scatter.4
